TPU v7x, 32 devices: a whole 2x2x4 slice. The times are simulated.
32 devices in a mesh: scan: 16 (over z, x, core), tile: 2 (over y).
Axes of the slice: x: 2, y: 2, z: 4, core: 2. Of those that a mesh axis runs over, the one named last changes fastest.
Arguments:
- probe_modes: float32 [12, 2, 128, 128], replicated, may hold values from -5 to 5
- patterns: float32 [128, 128, 128], P(('scan', 'tile')), may hold values from 0.005 to 300
- specimen: float32 [2, 2048, 512], P(None, 'scan', 'tile'), may hold values from -17.5 to 17.5
- offsets: int32 [128, 2], P(('scan', 'tile')), may hold values from -128 to 2048, as said below
Outputs:
- new_probe: float32 [12, 2, 128, 128], replicated
- new_specimen: float32 [2, 2048, 512], P(None, 'scan', 'tile')
Inputs may be any that keep to these rules, and one draw needn't show every extreme that they name: `offsets`: position p lies in aligned block b = p // 4, held by the device of scan index s = b // (the number of tile devices) and tile index t = b % (the number of tile devices); its row offset lies in s * 128 - 128 to s * 128 + 128, its column offset in t * 256 - 128 to t * 256 + 256, both ends included; in every block one position has its row offset at the lower end and its column offset at the upper end, and one has its row offset at the upper end.
All inputs are finite; a program needn't handle non-finite values.
Results may differ from a plain program's by a relative error of at most 0.0001.
Values sent between devices are 32-bit elements; how exact they have to be, the bound alone decides.
A program may use at most 64 MiB of HBM per device.

v0:
```python
import math
import jax
import jax.numpy as jnp
from jax import lax
from jax.sharding import PartitionSpec as P

NS_STEPS = 8
highest = lax.Precision.HIGHEST
light_floor = 0.05
object_reg = 0.5
probe_reg = 1.0
total_eps = 1e-06


def extended_2(array, sides, width):
    for axis, dim in sides:
        size, length = (lax.axis_size(axis), array.shape[dim])
        up = [(i, (i + 1) % size) for i in range(size - 1)]
        down = [(j, i) for i, j in up]
        last = lax.slice_in_dim(array, length - width, length, axis=dim)
        first = lax.slice_in_dim(array, 0, width, axis=dim)
        before = lax.ppermute(last, axis, up)
        after = lax.ppermute(first, axis, down)
        array = jnp.concatenate([before, array, after], axis=dim)
    return array


def dft_tables(detector):
    indices = jnp.arange(detector, dtype=jnp.int32)
    product = indices[:, None] * indices[None, :] % detector
    angles = -2.0 * math.pi / detector * product.astype(jnp.float32)
    norm_factor = 1.0 / math.sqrt(detector)
    return (jnp.cos(angles) * norm_factor, jnp.sin(angles) * norm_factor)


def complex_section(real_part, imag_part, table, direction, on_right):
    stacked = jnp.stack([real_part, imag_part])
    if on_right:
        products = jnp.einsum(
            "cmxy,yw->cmxw", stacked, table, precision=highest, preferred_element_type=jnp.float32
        )
        split_at = real_part.shape[-1]
        plain_re, twist_re = (products[0, :, :, :split_at], products[0, :, :, split_at:])
        plain_im, twist_im = (products[1, :, :, :split_at], products[1, :, :, split_at:])
    else:
        products = jnp.einsum(
            "wx,cmxy->cmwy", table, stacked, precision=highest, preferred_element_type=jnp.float32
        )
        split_at = real_part.shape[-2]
        plain_re, twist_re = (products[0, :, :split_at], products[0, :, split_at:])
        plain_im, twist_im = (products[1, :, :split_at], products[1, :, split_at:])
    return (plain_re - direction * twist_im, direction * twist_re + plain_im)


def newton_steps(gram_re, gram_im):
    mode_count = gram_re.shape[0]
    upper = jnp.concatenate([gram_re, -gram_im], axis=1)
    lower = jnp.concatenate([gram_im, gram_re], axis=1)
    embedded = jnp.concatenate([upper, lower], axis=0)
    frobenius = jnp.sqrt(jnp.sum(embedded * embedded))
    identity = jnp.eye(2 * mode_count, dtype=jnp.float32)
    current = embedded / frobenius
    inverse = identity
    for repeat in range(NS_STEPS):
        factor = 1.5 * identity - 0.5 * jnp.dot(
            inverse, current, precision=highest, preferred_element_type=jnp.float32
        )
        current = jnp.dot(current, factor, precision=highest, preferred_element_type=jnp.float32)
        inverse = jnp.dot(factor, inverse, precision=highest, preferred_element_type=jnp.float32)
    inverse = inverse / jnp.sqrt(frobenius)
    return (inverse[:mode_count, :mode_count], inverse[mode_count:, :mode_count])


def gram_parts(mode_rows):
    real_rows = mode_rows[0::2]
    imag_rows = mode_rows[1::2]
    gram_re = jnp.dot(
        real_rows, real_rows.T, precision=highest, preferred_element_type=jnp.float32
    ) + jnp.dot(imag_rows, imag_rows.T, precision=highest, preferred_element_type=jnp.float32)
    gram_im = jnp.dot(
        real_rows, imag_rows.T, precision=highest, preferred_element_type=jnp.float32
    ) - jnp.dot(imag_rows, real_rows.T, precision=highest, preferred_element_type=jnp.float32)
    return (gram_re, gram_im)


def orthonormal_rows(mode_rows, gram_re, gram_im, power_ratio):
    real_rows = mode_rows[0::2]
    imag_rows = mode_rows[1::2]
    mix_re, mix_im = newton_steps(gram_re, gram_im)
    ortho_re = jnp.dot(
        mix_re.T, real_rows, precision=highest, preferred_element_type=jnp.float32
    ) - jnp.dot(mix_im.T, imag_rows, precision=highest, preferred_element_type=jnp.float32)
    ortho_im = jnp.dot(
        mix_im.T, real_rows, precision=highest, preferred_element_type=jnp.float32
    ) + jnp.dot(mix_re.T, imag_rows, precision=highest, preferred_element_type=jnp.float32)
    weight = jnp.sqrt(power_ratio * jnp.diagonal(gram_re))
    joined = jnp.stack([ortho_re, ortho_im], axis=1) * weight[:, None, None]
    return joined.reshape(mode_rows.shape)


def global_totals(measured, modeled):
    return lax.psum((measured, modeled), ("scan", "tile"))


def fold_interior(frame_sum, folded, detector, block_rows, block_cols):
    rows_end = block_rows + 3 * detector
    cols_end = block_cols + 3 * detector
    centre_rows = slice(2 * detector, 2 * detector + block_rows)
    centre_cols = slice(2 * detector, 2 * detector + block_cols)
    interior = frame_sum[:, detector : detector + block_rows, detector : detector + block_cols]
    interior = interior.at[:, :detector, :].add(folded[:, :detector, centre_cols])
    interior = interior.at[:, block_rows - detector :, :].add(folded[:, rows_end:, centre_cols])
    interior = interior.at[:, :, :detector].add(folded[:, centre_rows, :detector])
    interior = interior.at[:, :, block_cols - detector :].add(folded[:, centre_rows, cols_end:])
    interior = interior.at[:, :detector, :detector].add(folded[:, :detector, :detector])
    interior = interior.at[:, :detector, block_cols - detector :].add(
        folded[:, :detector, cols_end:]
    )
    interior = interior.at[:, block_rows - detector :, :detector].add(
        folded[:, rows_end:, :detector]
    )
    interior = interior.at[:, block_rows - detector :, block_cols - detector :].add(
        folded[:, rows_end:, cols_end:]
    )
    return interior


def body(probe_modes, patterns, specimen, offsets):
    detector = probe_modes.shape[-1]
    mode_count = probe_modes.shape[0]
    block_rows = specimen.shape[1]
    block_cols = specimen.shape[2]
    position_count = patterns.shape[0]
    table_re, table_im = dft_tables(detector)
    right_table = jnp.concatenate([table_re, table_im], axis=1)
    left_table = jnp.concatenate([table_re, table_im], axis=0)
    probe_re = probe_modes[:, 0]
    probe_im = probe_modes[:, 1]
    probe_power = jnp.sum(probe_re * probe_re + probe_im * probe_im, axis=0)
    extended = extended_2(specimen, (("scan", 1), ("tile", 2)), detector)
    row_base = lax.axis_index("scan") * block_rows - detector
    col_base = lax.axis_index("tile") * block_cols - detector
    local_rows = offsets[:, 0] - row_base
    local_cols = offsets[:, 1] - col_base
    zero_index = jnp.zeros((), jnp.int32)
    channels = 3

    def patch_at(position):
        return lax.dynamic_slice(
            extended,
            (zero_index, local_rows[position], local_cols[position]),
            (2, detector, detector),
        )

    def one_position(position, running):
        grad_re, grad_im, light_sum, frame_sum, model_sum = running
        patch_now = patch_at(position)
        patch_re = patch_now[0]
        patch_im = patch_now[1]
        exit_re = probe_re * patch_re[None] - probe_im * patch_im[None]
        exit_im = probe_re * patch_im[None] + probe_im * patch_re[None]
        model_sum = model_sum + jnp.sum(exit_re * exit_re + exit_im * exit_im)
        half_re, half_im = complex_section(exit_re, exit_im, right_table, 1.0, True)
        far_re, far_im = complex_section(half_re, half_im, left_table, 1.0, False)
        model_light = jnp.sum(far_re * far_re + far_im * far_im, axis=0)
        factor = (
            jnp.sqrt(patterns[position]) / jnp.sqrt(jnp.maximum(model_light, light_floor)) - 1.0
        )
        back_re, back_im = complex_section(
            far_re * factor[None], far_im * factor[None], right_table, -1.0, True
        )
        change_re, change_im = complex_section(back_re, back_im, left_table, -1.0, False)
        grad_re = grad_re + patch_re[None] * change_re + patch_im[None] * change_im
        grad_im = grad_im + patch_re[None] * change_im - patch_im[None] * change_re
        light_sum = light_sum + patch_re * patch_re + patch_im * patch_im
        num_re = jnp.sum(probe_re * change_re + probe_im * change_im, axis=0)
        num_im = jnp.sum(probe_re * change_im - probe_im * change_re, axis=0)
        addition = jnp.stack([num_re, num_im, probe_power])
        row_at = local_rows[position]
        col_at = local_cols[position]
        previous = lax.dynamic_slice(
            frame_sum, (zero_index, row_at, col_at), (channels, detector, detector)
        )
        frame_sum = lax.dynamic_update_slice(
            frame_sum, previous + addition, (zero_index, row_at, col_at)
        )
        return (grad_re, grad_im, light_sum, frame_sum, model_sum)

    mode_zeros = jnp.zeros((mode_count, detector, detector), jnp.float32)
    frame_init = jnp.zeros(
        (channels, block_rows + 2 * detector, block_cols + 2 * detector), jnp.float32
    )
    initial = (
        mode_zeros,
        mode_zeros,
        jnp.zeros((detector, detector), jnp.float32),
        frame_init,
        jnp.zeros((), jnp.float32),
    )
    grad_re, grad_im, light_sum, frame_sum, model_sum = lax.fori_loop(
        0, position_count, one_position, initial
    )
    measured_all, model_all = global_totals(jnp.sum(patterns), model_sum)
    power_ratio = measured_all / (model_all + total_eps)
    folded = extended_2(frame_sum, (("scan", 1), ("tile", 2)), detector)
    interior = fold_interior(frame_sum, folded, detector, block_rows, block_cols)
    interior_num = interior[0:2]
    interior_light = interior[2]
    new_specimen = specimen + interior_num / (interior_light + object_reg)[None]
    grad_rows = jnp.stack([grad_re, grad_im], axis=1).reshape(2 * mode_count, -1)
    light_row = light_sum.reshape(1, -1)
    probe_rows = probe_modes.reshape(2 * mode_count, -1)
    grad_total, light_total = lax.psum((grad_rows, light_row), ("scan", "tile"))
    updated = probe_rows + grad_total / (light_total + probe_reg)
    gram_re, gram_im = gram_parts(updated)
    new_probe = orthonormal_rows(updated, gram_re, gram_im, power_ratio).reshape(probe_modes.shape)
    return (new_probe, new_specimen)


def solution(mesh):
    return jax.shard_map(
        body,
        mesh=mesh,
        in_specs=(
            P(),
            P(("scan", "tile"), None, None),
            P(None, "scan", "tile"),
            P(("scan", "tile"), None),
        ),
        out_specs=(P(), P(None, "scan", "tile")),
        check_vma=False,
    )
```

profile of v0, /device:TPU:0, one launch (start us, length us, event | category | flops | bytes accessed | tf_op | source)
XLA Modules:
  0.0 347.7 jit_solution(15075586222732396307)
XLA Ops:
  8.7 3.1 collective-permute-start
  12.8 2.1 add_reduce_fusion.3
  15.1 5.1 %collective-permute-start.2 = (f32[2,384,128]{2,1,0:T(8,128)S(1)}, f32[2,384,128]{2,1,0:T(8,128)S(1)}, u32[]{:S(2)}, u32[]{:S(2)}) collective-permute-start(f32[2,384,128]{2,1,0:T(8,128)S(1)} %get-tuple-element.611), channel_id=1, source_target_pairs={{0,1},{2,3},{4,5},{6,7},{8,9},{10,11},{12,13},{14,15},{16,17},{18,... | collective-permute-start | bytes 1179656 | tf_op jit(solution)/shard_map/ppermute | solution.py:22
  21.6 5.7 %collective-permute-done.2 = f32[2,384,128]{2,1,0:T(8,128)S(1)} collective-permute-done((f32[2,384,128]{2,1,0:T(8,128)S(1)}, f32[2,384,128]{2,1,0:T(8,128)S(1)}, u32[]{:S(2)}, u32[]{:S(2)}) %collective-permute-start.2) | collective-permute-done | bytes 393248 | tf_op jit(solution)/shard_map/ppermute | solution.py:22
  27.4 4.7 %collective-permute-done.3 = f32[2,384,128]{2,1,0:T(8,128)S(1)} collective-permute-done((f32[2,384,128]{2,1,0:T(8,128)S(1)}, f32[2,384,128]{2,1,0:T(8,128)S(1)}, u32[]{:S(2)}, u32[]{:S(2)}) %collective-permute-start.3) | collective-permute-done | bytes 393248 | tf_op jit(solution)/shard_map/ppermute | solution.py:23
  33.4 1.7 broadcast_in_dim.23
  35.1 113.1 %while.34 = (s32[]{:T(128)}, f32[12,128,128]{2,1,0:T(8,128)}, f32[12,128,128]{2,1,0:T(8,128)}, f32[128,128]{1,0:T(8,128)}, f32[3,384,512]{2,1,0:T(8,128)}, /*ind...) while((s32[]{:T(128)}, f32[12,128,128]{2,1,0:T(8,128)}, ...), condition=%wide.region_6.7_spmd.clone, body=%wide.region_1.6_spmd.clone.sunk | while | flops 4844257280 | bytes 53870996 | solution.py:200
  40.6 1.7 fusion.160
  42.5 2.7 fusion.162
  45.4 2.8 convolution_bitcast_fusion.4
  48.6 2.8 fusion.164
  51.6 2.7 convolution_bitcast_fusion.5
  58.8 2.8 dynamic_update_slice.12
  67.1 1.8 fusion.160
  69.1 2.7 fusion.162
  72.0 2.8 convolution_bitcast_fusion.4
  75.2 2.8 fusion.164
  78.2 2.7 convolution_bitcast_fusion.5
  82.9 2.8 fusion.166
  86.9 2.8 dynamic_update_slice.12
  95.2 1.8 fusion.160
  97.2 2.7 fusion.162
  100.1 2.8 convolution_bitcast_fusion.4
  103.3 2.8 fusion.164
  106.3 2.7 convolution_bitcast_fusion.5
  111.0 2.8 fusion.166
  115.0 4.0 %dynamic_update_slice.12 = f32[3,384,512]{2,1,0:T(8,128)} dynamic-update-slice(f32[3,384,512]{2,1,0:T(8,128)} %get-tuple-element.770, f32[3,128,128]{2,1,0:T(8,128)S(1)} %maximum_add_fusion.2, s32[]{:T(128)} %constant.327.clone.1..sunk, s32[]{:T(128)S(6)} %select_n.67, s32[]{:T(128)S(6)} %select_n.68) | dynamic-update-slice | bytes 393220 | tf_op jit(solution)/shard_map/while/body/eval_jaxpr/dynamic_update_slice | solution.py:184
  124.5 1.8 fusion.160
  126.5 2.7 fusion.162
  129.4 2.8 convolution_bitcast_fusion.4
  132.6 2.8 fusion.164
  135.6 2.7 convolution_bitcast_fusion.5
  140.3 2.8 fusion.166
  144.3 4.0 %dynamic_update_slice.12 = f32[3,384,512]{2,1,0:T(8,128)} dynamic-update-slice(f32[3,384,512]{2,1,0:T(8,128)} %get-tuple-element.770, f32[3,128,128]{2,1,0:T(8,128)S(1)} %maximum_add_fusion.2, s32[]{:T(128)} %constant.327.clone.1..sunk, s32[]{:T(128)S(6)} %select_n.67, s32[]{:T(128)S(6)} %select_n.68) | dynamic-update-slice | bytes 393220 | tf_op jit(solution)/shard_map/while/body/eval_jaxpr/dynamic_update_slice | solution.py:184
  148.3 2.8 fusion.66
  151.1 3.7 %collective-permute-start.4 = (f32[3,128,512]{2,1,0:T(8,128)}, f32[3,128,512]{2,1,0:T(8,128)S(1)}, u32[]{:S(2)}, u32[]{:S(2)}) collective-permute-start(f32[3,128,512]{2,1,0:T(8,128)} %get-tuple-element.607), channel_id=1, source_target_pairs={{0,2},{2,4},{4,6},{6,8},{8,10},{10,12},{12,14},{14,16},{16,18},{18... | collective-permute-start | bytes 2359304 | tf_op jit(solution)/shard_map/ppermute | solution.py:22
  156.1 1.7 reduce_sum.93
  158.0 2.1 copy.40
  160.1 51.6 %all-reduce = (f32[]{:T(128)}, f32[]{:T(128)}) all-reduce(f32[]{:T(128)} %reduce_sum.93, f32[]{:T(128)} %get-tuple-element.473), channel_id=1, replica_groups=mesh['scan'=16,'tile'=2] {'scan','tile'}, use_global_device_ids=true, to_apply=%region_11.12 | all-reduce | flops 2 | bytes 16 | tf_op jit(solution)/shard_map/psum | solution.py:102
  213.1 2.1 constant_dynamic-update-slice_fusion.4
  219.0 6.4 %collective-permute-start.6 = (f32[3,640,128]{2,1,0:T(8,128)}, f32[3,640,128]{2,1,0:T(8,128)}, u32[]{:S(2)}, u32[]{:S(2)}) collective-permute-start(f32[3,640,128]{2,1,0:T(8,128)} %get-tuple-element.606), channel_id=1, source_target_pairs={{0,1},{2,3},{4,5},{6,7},{8,9},{10,11},{12,13},{14,15},{16,17},{18,... | collective-permute-start | bytes 2949128 | tf_op jit(solution)/shard_map/ppermute | solution.py:22
  226.7 70.5 %all-reduce.4.cloned.1.call-done = (f32[24,16384]{1,0:T(8,128)}, f32[1,16384]{1,0:T(1,128)}) async-done(((f32[24,16384]{1,0:T(8,128)}, f32[1,16384]{1,0:T(1,128)}), (f32[24,16384]{1,0:T(8,128)}, f32[1,16384]{1,0:T(1,128)})) %all-reduce.4.cloned.1.call-update) | async-done | bytes 1638416 | tf_op jit(solution)/shard_map/psum | solution.py:213
  298.1 3.5 %bitcast_add_fusion = f32[24,16384]{1,0:T(8,128)} fusion(f32[3,8,128,128]{3,2,1,0:T(8,128)S(1)} %bitcast.192, f32[24,16384]{1,0:T(8,128)} %get-tuple-element.588, f32[16384]{0:T(1024)S(1)} %bitcast.201), kind=kLoop, calls=%fused_computation.67 | loop fusion | flops 786432 | bytes 4784128 | tf_op jit(solution)/shard_map/add | solution.py:214
  301.6 5.7 %slice.446 = f32[12,16384]{1,0:T(8,128)S(1)} slice(f32[24,16384]{1,0:T(8,128)} %bitcast_add_fusion), slice={[1:24:2], [0:16384:1]} | slice | bytes 1572864 | tf_op jit(solution)/shard_map/slice | solution.py:76
  307.3 5.7 %slice.445 = f32[12,16384]{1,0:T(8,128)S(1)} slice(f32[24,16384]{1,0:T(8,128)} %bitcast_add_fusion), slice={[0:24:2], [0:16384:1]} | slice | bytes 1572864 | tf_op jit(solution)/shard_map/slice | solution.py:75
  324.1 2.0 fusion.56
  326.1 2.0 fusion.60
  328.8 2.4 convolution_subtract_fusion
  (162 shorter events, 57.3 us)
Async XLA Ops:
  7.2 7.8 %copy-start.10 = (f32[2,128,256]{2,1,0:T(8,128)S(1)}, f32[2,128,256]{2,1,0:T(8,128)}, u32[]{:S(2)}) copy-start(f32[2,128,256]{2,1,0:T(8,128)} %param.28) | copy-start | bytes 786436
  7.2 290.0 %all-reduce.4.cloned.1.call-start = ((), (), s32[]{:S(2)}) async-start(), calls=%async_computation | async-start | bytes 3276800 | tf_op jit(solution)/shard_map/psum | solution.py:213
  7.2 7.8 %collective-permute-start.1 = (f32[2,128,256]{2,1,0:T(8,128)}, f32[2,128,256]{2,1,0:T(8,128)S(1)}, u32[]{:S(2)}, u32[]{:S(2)}) collective-permute-start(f32[2,128,256]{2,1,0:T(8,128)} %param.28), channel_id=1, source_target_pairs={{2,0},{4,2},{6,4},{8,6},{10,8},{12,10},{14,12},{16,14},{18,16},{20... | collective-permute-start | bytes 786440 | tf_op jit(solution)/shard_map/ppermute | solution.py:23
  8.7 6.3 %collective-permute-start = (f32[2,128,256]{2,1,0:T(8,128)}, f32[2,128,256]{2,1,0:T(8,128)S(1)}, u32[]{:S(2)}, u32[]{:S(2)}) collective-permute-start(f32[2,128,256]{2,1,0:T(8,128)} %param.28), channel_id=1, source_target_pairs={{0,2},{2,4},{4,6},{6,8},{8,10},{10,12},{12,14},{14,16},{16,18},{18... | collective-permute-start | bytes 786440 | tf_op jit(solution)/shard_map/ppermute | solution.py:22
  15.0 6.5 %copy-start.2 = (f32[12,2,128,128]{3,2,1,0:T(8,128)S(1)}, f32[12,2,128,128]{3,2,1,0:T(8,128)}, u32[]{:S(2)}) copy-start(f32[12,2,128,128]{3,2,1,0:T(8,128)} %param.26) | copy-start | bytes 4718596
  15.1 12.2 %collective-permute-start.2 = (f32[2,384,128]{2,1,0:T(8,128)S(1)}, f32[2,384,128]{2,1,0:T(8,128)S(1)}, u32[]{:S(2)}, u32[]{:S(2)}) collective-permute-start(f32[2,384,128]{2,1,0:T(8,128)S(1)} %get-tuple-element.611), channel_id=1, source_target_pairs={{0,1},{2,3},{4,5},{6,7},{8,9},{10,11},{12,13},{14,15},{16,17},{18,... | collective-permute-start | bytes 1179656 | tf_op jit(solution)/shard_map/ppermute | solution.py:22
  20.2 11.9 %collective-permute-start.3 = (f32[2,384,128]{2,1,0:T(8,128)S(1)}, f32[2,384,128]{2,1,0:T(8,128)S(1)}, u32[]{:S(2)}, u32[]{:S(2)}) collective-permute-start(f32[2,384,128]{2,1,0:T(8,128)S(1)} %get-tuple-element.612), channel_id=1, source_target_pairs={{1,0},{3,2},{5,4},{7,6},{9,8},{11,10},{13,12},{15,14},{17,16},{19,... | collective-permute-start | bytes 1179656 | tf_op jit(solution)/shard_map/ppermute | solution.py:23
  56.2 1.4 copy-start.4
  56.3 1.4 copy-start.5
  82.8 2.8 copy-start.4
  82.9 2.8 copy-start.5
  111.0 2.8 copy-start.4
  111.0 2.8 copy-start.5
  140.2 2.8 copy-start.4
  140.2 2.8 copy-start.5
  148.2 9.6 %copy-start = (f32[12,128,128]{2,1,0:T(8,128)S(1)}, f32[12,128,128]{2,1,0:T(8,128)}, u32[]{:S(2)}) copy-start(f32[12,128,128]{2,1,0:T(8,128)} %get-tuple-element.471) | copy-start | bytes 2359300
  148.2 9.6 %copy-start.1 = (f32[12,128,128]{2,1,0:T(8,128)S(1)}, f32[12,128,128]{2,1,0:T(8,128)}, u32[]{:S(2)}) copy-start(f32[12,128,128]{2,1,0:T(8,128)} %get-tuple-element.470) | copy-start | bytes 2359300
  151.1 61.9 %collective-permute-start.4 = (f32[3,128,512]{2,1,0:T(8,128)}, f32[3,128,512]{2,1,0:T(8,128)S(1)}, u32[]{:S(2)}, u32[]{:S(2)}) collective-permute-start(f32[3,128,512]{2,1,0:T(8,128)} %get-tuple-element.607), channel_id=1, source_target_pairs={{0,2},{2,4},{4,6},{6,8},{8,10},{10,12},{12,14},{14,16},{16,18},{18... | collective-permute-start | bytes 2359304 | tf_op jit(solution)/shard_map/ppermute | solution.py:22
  154.8 60.4 %collective-permute-start.5 = (f32[3,128,512]{2,1,0:T(8,128)}, f32[3,128,512]{2,1,0:T(8,128)S(1)}, u32[]{:S(2)}, u32[]{:S(2)}) collective-permute-start(f32[3,128,512]{2,1,0:T(8,128)} %get-tuple-element.608), channel_id=1, source_target_pairs={{2,0},{4,2},{6,4},{8,6},{10,8},{12,10},{14,12},{16,14},{18,16},{20... | collective-permute-start | bytes 2359304 | tf_op jit(solution)/shard_map/ppermute | solution.py:23
  213.0 2.2 copy-start.7
  215.2 1.0 copy-start.9
  216.2 9.3 %copy-start.8 = (f32[3,128,512]{2,1,0:T(8,128)S(1)}, f32[3,128,512]{2,1,0:T(8,128)}, u32[]{:S(2)}) copy-start(f32[3,128,512]{2,1,0:T(8,128)} %copy-done.7) | copy-start | bytes 2359300
  217.6 80.4 %copy-start.3 = (f32[12,2,128,128]{3,2,1,0:T(8,128)S(1)}, f32[12,2,128,128]{3,2,1,0:T(8,128)}, u32[]{:S(2)}) copy-start(f32[12,2,128,128]{3,2,1,0:T(8,128)} %param.26) | copy-start | bytes 4718596
  217.6 117.6 %collective-permute-start.7 = (f32[3,640,128]{2,1,0:T(8,128)}, f32[3,640,128]{2,1,0:T(8,128)}, u32[]{:S(2)}, u32[]{:S(2)}) collective-permute-start(f32[3,640,128]{2,1,0:T(8,128)} %get-tuple-element.605), channel_id=1, source_target_pairs={{1,0},{3,2},{5,4},{7,6},{9,8},{11,10},{13,12},{15,14},{17,16},{19,... | collective-permute-start | bytes 2949128 | tf_op jit(solution)/shard_map/ppermute | solution.py:23
  219.0 115.2 %collective-permute-start.6 = (f32[3,640,128]{2,1,0:T(8,128)}, f32[3,640,128]{2,1,0:T(8,128)}, u32[]{:S(2)}, u32[]{:S(2)}) collective-permute-start(f32[3,640,128]{2,1,0:T(8,128)} %get-tuple-element.606), channel_id=1, source_target_pairs={{0,1},{2,3},{4,5},{6,7},{8,9},{10,11},{12,13},{14,15},{16,17},{18,... | collective-permute-start | bytes 2949128 | tf_op jit(solution)/shard_map/ppermute | solution.py:22
  328.8 2.4 copy-start.6
  335.2 5.0 %copy-start.11 = (f32[2,128,256]{2,1,0:T(8,128)S(1)}, f32[2,128,256]{2,1,0:T(8,128)}, u32[]{:S(2)}) copy-start(f32[2,128,256]{2,1,0:T(8,128)} %param.28) | copy-start | bytes 786436
Sparse Core Ops, SparseCore 0:
  160.2 136.8 all-reduce.3
where the time goes:
time: 350 us; the launch traced here: 348 us
  waiting for transfers between devices  81 us (23%)
  matrix products  60.7 us (17%)
  blocking collectives  51.6 us (15%)
  other arithmetic  51.5 us (15%)
  local copies, waits for them, and re-layouts  46.2 us (13%)
  starting transfers between devices  23.7 us (7%)
  between operations  16.5 us (5%)
  loops' own time  16.4 us (5%)
    psum x1, waiting for transfers between devices, body(): grad_total, light_total = lax.psum((grad_rows, light_row), ('scan', 'tile'))  70.5 us
    psum x1, blocking collectives, global_totals(): return lax.psum((measured, modeled), ('scan', 'tile'))  51.6 us
    dot_general x8, matrix products, complex_section(): jnp.einsum('wx,cmxy->cmwy', table, stacked, precision=highest, preferred_...  22 us
    dot_general x8, matrix products, complex_section(): jnp.einsum('cmxy,yw->cmxw', stacked, table, precision=highest, preferred_...  21.8 us
    ppermute x4, starting transfers between devices, extended_2(): before = lax.ppermute(last, axis, up)  18.2 us
    another operation x1, loops' own time, body(): lax.fori_loop(0, position_count, one_position, initial)  16.4 us
    dynamic_update_slice x4, local copies, waits for them, and re-layouts, one_position(): lax.dynamic_update_slice(frame_sum, previous + addition, (zero_index, row...  13.6 us
    sub x4, other arithmetic, one_position(): grad_im = grad_im + patch_re[None] * change_im - patch_im[None] * change_re  9.88 us
  transfers between devices with their start and end apart: 9, of which 3 were waited for; matrix products, arithmetic and copies ran while one was open for 14% of the time, Pallas kernels for 0%

commit v1 on v0

--- a/solution.py
+++ b/solution.py
@@ -210,7 +210,7 @@
     grad_rows = jnp.stack([grad_re, grad_im], axis=1).reshape(2 * mode_count, -1)
     light_row = light_sum.reshape(1, -1)
     probe_rows = probe_modes.reshape(2 * mode_count, -1)
-    grad_total, light_total = lax.psum((grad_rows, light_row), ("scan", "tile"))
+    grad_total, light_total = lax.psum(lax.psum((grad_rows, light_row), "tile"), "scan")
     updated = probe_rows + grad_total / (light_total + probe_reg)
     gram_re, gram_im = gram_parts(updated)
     new_probe = orthonormal_rows(updated, gram_re, gram_im, power_ratio).reshape(probe_modes.shape)

time: 350 us -> 389 us (1.11)
  blocking collectives: 51.6 us -> 73.1 us
  waiting for transfers between devices: 81 us -> 101 us
  starting transfers between devices: 23.7 us -> 19.6 us
    psum x1, blocking collectives: 51.6 us -> 73.1 us  [global_totals(): return lax.psum((measured, modeled), ('scan', 'tile'))]
    psum x1 -> x2, waiting for transfers between devices: 70.5 us -> 89.1 us  [the longest x1 89.1 us: body(): lax.psum(lax.psum((grad_rows, light_row), 'tile'), 'scan')]
    ppermute x4, starting transfers between devices: 18.2 us -> 14.2 us  [extended_2(): before = lax.ppermute(last, axis, up)]
  transfers between devices with their start and end apart: 9 -> 10, of which waited for: 3 -> 4; matrix products, arithmetic and copies ran while one was open for 14% -> 5% of each run, Pallas kernels for 0% -> 0%
where the time goes in v1:
time: 389 us; the launch traced here: 387 us
  waiting for transfers between devices  101 us (26%)
  blocking collectives  73.1 us (19%)
  matrix products  59.7 us (15%)
  other arithmetic  50.5 us (13%)
  local copies, waits for them, and re-layouts  46.8 us (12%)
  starting transfers between devices  19.6 us (5%)
  loops' own time  19.6 us (5%)
  between operations  16.6 us (4%)
    psum x1, waiting for transfers between devices, body(): lax.psum(lax.psum((grad_rows, light_row), 'tile'), 'scan')  89.1 us
    psum x1, blocking collectives, global_totals(): return lax.psum((measured, modeled), ('scan', 'tile'))  73.1 us
    dot_general x8, matrix products, complex_section(): jnp.einsum('wx,cmxy->cmwy', table, stacked, precision=highest, preferred_...  21.9 us
    dot_general x8, matrix products, complex_section(): jnp.einsum('cmxy,yw->cmxw', stacked, table, precision=highest, preferred_...  21.8 us
    another operation x1, loops' own time, body(): lax.fori_loop(0, position_count, one_position, initial)  19.6 us
    ppermute x4, starting transfers between devices, extended_2(): before = lax.ppermute(last, axis, up)  14.2 us
    dynamic_update_slice x4, local copies, waits for them, and re-layouts, one_position(): lax.dynamic_update_slice(frame_sum, previous + addition, (zero_index, row...  13.6 us
    sub x4, other arithmetic, one_position(): grad_im = grad_im + patch_re[None] * change_im - patch_im[None] * change_re  9.93 us
  transfers between devices with their start and end apart: 10, of which 4 were waited for; matrix products, arithmetic and copies ran while one was open for 5% of the time, Pallas kernels for 0%

profile of v1, /device:TPU:0, one launch (start us, length us, event | category | flops | bytes accessed | tf_op | source)
XLA Modules:
  0.0 387.0 jit_solution(14822037529138080412)
XLA Ops:
  8.7 3.1 collective-permute-start
  12.8 2.1 add_reduce_fusion.3
  15.1 5.1 %collective-permute-start.2 = (f32[2,384,128]{2,1,0:T(8,128)S(1)}, f32[2,384,128]{2,1,0:T(8,128)S(1)}, u32[]{:S(2)}, u32[]{:S(2)}) collective-permute-start(f32[2,384,128]{2,1,0:T(8,128)S(1)} %get-tuple-element.613), channel_id=1, source_target_pairs={{0,1},{2,3},{4,5},{6,7},{8,9},{10,11},{12,13},{14,15},{16,17},{18,... | collective-permute-start | bytes 1179656 | tf_op jit(solution)/shard_map/ppermute | solution.py:22
  21.7 5.7 %collective-permute-done.2 = f32[2,384,128]{2,1,0:T(8,128)S(1)} collective-permute-done((f32[2,384,128]{2,1,0:T(8,128)S(1)}, f32[2,384,128]{2,1,0:T(8,128)S(1)}, u32[]{:S(2)}, u32[]{:S(2)}) %collective-permute-start.2) | collective-permute-done | bytes 393248 | tf_op jit(solution)/shard_map/ppermute | solution.py:22
  27.3 4.7 %collective-permute-done.3 = f32[2,384,128]{2,1,0:T(8,128)S(1)} collective-permute-done((f32[2,384,128]{2,1,0:T(8,128)S(1)}, f32[2,384,128]{2,1,0:T(8,128)S(1)}, u32[]{:S(2)}, u32[]{:S(2)}) %collective-permute-start.3) | collective-permute-done | bytes 393248 | tf_op jit(solution)/shard_map/ppermute | solution.py:23
  33.4 1.7 broadcast_in_dim.23
  35.1 116.9 %while.34 = (s32[]{:T(128)}, f32[12,128,128]{2,1,0:T(8,128)}, f32[12,128,128]{2,1,0:T(8,128)}, f32[128,128]{1,0:T(8,128)}, f32[3,384,512]{2,1,0:T(8,128)}, /*ind...) while((s32[]{:T(128)}, f32[12,128,128]{2,1,0:T(8,128)}, ...), condition=%wide.region_6.7_spmd.clone, body=%wide.region_1.6_spmd.clone.sunk | while | flops 4844257280 | bytes 53870996 | solution.py:200
  41.4 1.7 fusion.160
  43.3 2.7 fusion.162
  46.2 2.8 convolution_bitcast_fusion.4
  49.4 2.8 fusion.164
  52.4 2.7 convolution_bitcast_fusion.5
  59.7 2.8 dynamic_update_slice.12
  68.9 1.8 fusion.160
  70.8 2.7 fusion.162
  73.7 2.8 convolution_bitcast_fusion.4
  76.9 2.8 fusion.164
  79.9 2.7 convolution_bitcast_fusion.5
  84.7 2.8 fusion.166
  88.7 2.8 dynamic_update_slice.12
  97.9 1.8 fusion.160
  99.9 2.7 fusion.162
  102.8 2.8 convolution_bitcast_fusion.4
  106.0 2.8 fusion.164
  108.9 2.7 convolution_bitcast_fusion.5
  113.8 2.8 fusion.166
  117.8 4.0 %dynamic_update_slice.12 = f32[3,384,512]{2,1,0:T(8,128)} dynamic-update-slice(f32[3,384,512]{2,1,0:T(8,128)} %get-tuple-element.772, f32[3,128,128]{2,1,0:T(8,128)S(1)} %maximum_add_fusion.2, s32[]{:T(128)} %constant.327.clone.1..sunk, s32[]{:T(128)S(6)} %select_n.67, s32[]{:T(128)S(6)} %select_n.68) | dynamic-update-slice | bytes 393220 | tf_op jit(solution)/shard_map/while/body/eval_jaxpr/dynamic_update_slice | solution.py:184
  128.1 1.8 fusion.160
  130.1 2.7 fusion.162
  133.0 2.8 convolution_bitcast_fusion.4
  136.2 2.8 fusion.164
  139.2 2.7 convolution_bitcast_fusion.5
  144.0 2.8 fusion.166
  148.0 4.0 %dynamic_update_slice.12 = f32[3,384,512]{2,1,0:T(8,128)} dynamic-update-slice(f32[3,384,512]{2,1,0:T(8,128)} %get-tuple-element.772, f32[3,128,128]{2,1,0:T(8,128)S(1)} %maximum_add_fusion.2, s32[]{:T(128)} %constant.327.clone.1..sunk, s32[]{:T(128)S(6)} %select_n.67, s32[]{:T(128)S(6)} %select_n.68) | dynamic-update-slice | bytes 393220 | tf_op jit(solution)/shard_map/while/body/eval_jaxpr/dynamic_update_slice | solution.py:184
  152.0 2.9 fusion.66
  154.9 3.7 collective-permute-start.4
  160.2 2.1 copy.40
  164.1 1.5 collective-permute-done.5
  168.3 2.4 collective-permute-start.6
  172.0 1.7 reduce_sum.93
  173.7 73.1 %all-reduce = (f32[]{:T(128)}, f32[]{:T(128)}) all-reduce(f32[]{:T(128)} %reduce_sum.93, f32[]{:T(128)} %get-tuple-element.473), channel_id=1, replica_groups=mesh['scan'=16,'tile'=2] {'scan','tile'}, use_global_device_ids=true, to_apply=%region_13.14 | all-reduce | flops 2 | bytes 16 | tf_op jit(solution)/shard_map/psum | solution.py:102
  256.2 89.1 %all-reduce.6.cloned.1.call-done = (f32[24,16384]{1,0:T(8,128)}, f32[1,16384]{1,0:T(1,128)}) async-done(((f32[24,16384]{1,0:T(8,128)}, f32[1,16384]{1,0:T(1,128)}), (f32[24,16384]{1,0:T(8,128)}, f32[1,16384]{1,0:T(1,128)})) %all-reduce.6.cloned.1.call-update) | async-done | bytes 1638416 | tf_op jit(solution)/shard_map/psum | solution.py:213
  346.2 2.4 bitcast_add_fusion
  349.7 4.6 %slice.446 = f32[12,16384]{1,0:T(8,128)S(1)} slice(f32[24,16384]{1,0:T(8,128)S(1)} %bitcast_add_fusion), slice={[1:24:2], [0:16384:1]} | slice | bytes 1572864 | tf_op jit(solution)/shard_map/slice | solution.py:76
  354.3 5.7 %slice.445 = f32[12,16384]{1,0:T(8,128)S(1)} slice(f32[24,16384]{1,0:T(8,128)} %copy-done.5), slice={[0:24:2], [0:16384:1]} | slice | bytes 1572864 | tf_op jit(solution)/shard_map/slice | solution.py:75
  363.0 1.6 convolution_add_fusion.1
  372.2 2.0 fusion.60
  374.9 2.3 convolution_subtract_fusion
  (161 shorter events, 60.6 us)
Async XLA Ops:
  7.2 7.8 %copy-start.8 = (f32[2,128,256]{2,1,0:T(8,128)S(1)}, f32[2,128,256]{2,1,0:T(8,128)}, u32[]{:S(2)}) copy-start(f32[2,128,256]{2,1,0:T(8,128)} %param.28) | copy-start | bytes 786436
  7.2 242.0 %all-reduce.8.cloned.1.call-start = ((), (), s32[]{:S(2)}) async-start(), calls=%async_computation.1 | async-start | bytes 3276800 | tf_op jit(solution)/shard_map/psum | solution.py:213
  7.2 7.8 %collective-permute-start.1 = (f32[2,128,256]{2,1,0:T(8,128)}, f32[2,128,256]{2,1,0:T(8,128)S(1)}, u32[]{:S(2)}, u32[]{:S(2)}) collective-permute-start(f32[2,128,256]{2,1,0:T(8,128)} %param.28), channel_id=1, source_target_pairs={{2,0},{4,2},{6,4},{8,6},{10,8},{12,10},{14,12},{16,14},{18,16},{20... | collective-permute-start | bytes 786440 | tf_op jit(solution)/shard_map/ppermute | solution.py:23
  8.7 6.3 %collective-permute-start = (f32[2,128,256]{2,1,0:T(8,128)}, f32[2,128,256]{2,1,0:T(8,128)S(1)}, u32[]{:S(2)}, u32[]{:S(2)}) collective-permute-start(f32[2,128,256]{2,1,0:T(8,128)} %param.28), channel_id=1, source_target_pairs={{0,2},{2,4},{4,6},{6,8},{8,10},{10,12},{12,14},{14,16},{16,18},{18... | collective-permute-start | bytes 786440 | tf_op jit(solution)/shard_map/ppermute | solution.py:22
  15.0 6.5 %copy-start.3 = (f32[12,2,128,128]{3,2,1,0:T(8,128)S(1)}, f32[12,2,128,128]{3,2,1,0:T(8,128)}, u32[]{:S(2)}) copy-start(f32[12,2,128,128]{3,2,1,0:T(8,128)} %param.26) | copy-start | bytes 4718596
  15.1 12.2 %collective-permute-start.2 = (f32[2,384,128]{2,1,0:T(8,128)S(1)}, f32[2,384,128]{2,1,0:T(8,128)S(1)}, u32[]{:S(2)}, u32[]{:S(2)}) collective-permute-start(f32[2,384,128]{2,1,0:T(8,128)S(1)} %get-tuple-element.613), channel_id=1, source_target_pairs={{0,1},{2,3},{4,5},{6,7},{8,9},{10,11},{12,13},{14,15},{16,17},{18,... | collective-permute-start | bytes 1179656 | tf_op jit(solution)/shard_map/ppermute | solution.py:22
  20.2 11.9 %collective-permute-start.3 = (f32[2,384,128]{2,1,0:T(8,128)S(1)}, f32[2,384,128]{2,1,0:T(8,128)S(1)}, u32[]{:S(2)}, u32[]{:S(2)}) collective-permute-start(f32[2,384,128]{2,1,0:T(8,128)S(1)} %get-tuple-element.614), channel_id=1, source_target_pairs={{1,0},{3,2},{5,4},{7,6},{9,8},{11,10},{13,12},{15,14},{17,16},{19,... | collective-permute-start | bytes 1179656 | tf_op jit(solution)/shard_map/ppermute | solution.py:23
  57.2 1.5 copy-start.6
  57.2 1.5 copy-start.7
  84.7 2.9 copy-start.6
  84.7 2.8 copy-start.7
  113.7 2.9 copy-start.6
  113.8 2.8 copy-start.7
  144.0 2.9 copy-start.6
  144.0 2.8 copy-start.7
  152.0 7.9 %copy-start = (f32[12,128,128]{2,1,0:T(8,128)S(1)}, f32[12,128,128]{2,1,0:T(8,128)}, u32[]{:S(2)}) copy-start(f32[12,128,128]{2,1,0:T(8,128)} %get-tuple-element.471) | copy-start | bytes 2359300
  152.0 7.9 %copy-start.1 = (f32[12,128,128]{2,1,0:T(8,128)S(1)}, f32[12,128,128]{2,1,0:T(8,128)}, u32[]{:S(2)}) copy-start(f32[12,128,128]{2,1,0:T(8,128)} %get-tuple-element.470) | copy-start | bytes 2359300
  154.9 7.5 %collective-permute-start.4 = (f32[3,128,512]{2,1,0:T(8,128)}, f32[3,128,512]{2,1,0:T(8,128)S(1)}, u32[]{:S(2)}, u32[]{:S(2)}) collective-permute-start(f32[3,128,512]{2,1,0:T(8,128)} %get-tuple-element.609), channel_id=1, source_target_pairs={{0,2},{2,4},{4,6},{6,8},{8,10},{10,12},{12,14},{14,16},{16,18},{18... | collective-permute-start | bytes 2359304 | tf_op jit(solution)/shard_map/ppermute | solution.py:22
  158.5 7.1 %collective-permute-start.5 = (f32[3,128,512]{2,1,0:T(8,128)}, f32[3,128,512]{2,1,0:T(8,128)}, u32[]{:S(2)}, u32[]{:S(2)}) collective-permute-start(f32[3,128,512]{2,1,0:T(8,128)} %get-tuple-element.610), channel_id=1, source_target_pairs={{2,0},{4,2},{6,4},{8,6},{10,8},{12,10},{14,12},{16,14},{18,16},{20... | collective-permute-start | bytes 2359304 | tf_op jit(solution)/shard_map/ppermute | solution.py:23
  162.2 1.7 copy-start.2
  162.3 183.0 %all-reduce.6.cloned.1.call-start = ((), (), s32[]{:S(2)}) async-start(), calls=%async_computation | async-start | bytes 3276800 | tf_op jit(solution)/shard_map/psum | solution.py:213
  168.3 81.0 %collective-permute-start.6 = (f32[3,640,128]{2,1,0:T(8,128)}, f32[3,640,128]{2,1,0:T(8,128)}, u32[]{:S(2)}, u32[]{:S(2)}) collective-permute-start(f32[3,640,128]{2,1,0:T(8,128)} %get-tuple-element.608), channel_id=1, source_target_pairs={{0,1},{2,3},{4,5},{6,7},{8,9},{10,11},{12,13},{14,15},{16,17},{18,... | collective-permute-start | bytes 2949128 | tf_op jit(solution)/shard_map/ppermute | solution.py:22
  170.7 79.6 %collective-permute-start.7 = (f32[3,640,128]{2,1,0:T(8,128)}, f32[3,640,128]{2,1,0:T(8,128)}, u32[]{:S(2)}, u32[]{:S(2)}) collective-permute-start(f32[3,640,128]{2,1,0:T(8,128)} %get-tuple-element.607), channel_id=1, source_target_pairs={{1,0},{3,2},{5,4},{7,6},{9,8},{11,10},{13,12},{15,14},{17,16},{19,... | collective-permute-start | bytes 2949128 | tf_op jit(solution)/shard_map/ppermute | solution.py:23
  250.2 5.2 %copy-start.9 = (f32[2,128,256]{2,1,0:T(8,128)S(1)}, f32[2,128,256]{2,1,0:T(8,128)}, u32[]{:S(2)}) copy-start(f32[2,128,256]{2,1,0:T(8,128)} %param.28) | copy-start | bytes 786436
  252.3 93.9 %copy-start.4 = (f32[12,2,128,128]{3,2,1,0:T(8,128)S(1)}, f32[12,2,128,128]{3,2,1,0:T(8,128)}, u32[]{:S(2)}) copy-start(f32[12,2,128,128]{3,2,1,0:T(8,128)} %param.26) | copy-start | bytes 4718596
  348.6 1.1 copy-start.5
Sparse Core Ops, SparseCore 0:
  162.4 70.1 all-reduce.7
  249.4 95.8 all-reduce.5
